TPU v7x, 512 devices: a whole 4x8x8 slice. The times are simulated.
512 devices in a mesh: pool: 16 (over z, y_hi), fft: 32 (over x, y_lo, core).
Axes of the slice: x: 4, y: 8 (y_hi: 2, y_lo: 4; y = y_hi * 4 + y_lo), z: 8, core: 2. Of those that a mesh axis runs over, the one named last changes fastest.
Arguments:
- orbitals: bfloat16 [16, 2, 1, 160, 25600], P('pool', None, None, 'fft'), may hold values from -6 to 6
- stick_map: int32 [16000], replicated, may hold values from -1 to 25599, as said below
- kpoint_grid: int32 [16, 3], replicated, may hold values from 0 to 3, as said below
Outputs:
- exchange_action: bfloat16 [16, 2, 1, 160, 25600], P('pool', None, None, 'fft')
Inputs may be any that keep to these rules, and one draw needn't show every extreme that they name: `stick_map`: entries other than -1 are distinct columns. Slots come in blocks of 500 per index of fft; in each block at least half of the slots are live, and in every draw some block has all 500 live. `kpoint_grid`: rows are distinct.
All inputs are finite; a program needn't handle non-finite values.
Results may differ from a plain program's by a relative error of at most 0.011.
Values may be sent and summed in bfloat16 or wider, within the bound.
A program may use at most 64 MiB of HBM per device.

v0:
```python
import math
import jax
import jax.numpy as jnp
from jax import lax
from jax.sharding import PartitionSpec as P

NG = 160
KMESH = 4
SPACING_BOHR = 0.1875
SCREENING = 0.106


def shifted(value, axis, steps):
    count = lax.axis_size(axis)
    pairs = [(source, (source + steps) % count) for source in range(count)]
    return lax.ppermute(value, axis, pairs)


def dft_table(grid_size, orientation):
    positions = jnp.arange(grid_size, dtype=jnp.int32)
    product = positions[:, None] * positions[None, :] % grid_size
    angle = product.astype(jnp.float32) * (2.0 * math.pi / grid_size)
    cosine = jnp.cos(angle)
    sine = orientation * jnp.sin(angle)
    upper = jnp.stack([cosine, sine], axis=1)
    lower = jnp.stack([-sine, cosine], axis=1)
    return jnp.stack([upper, lower], axis=0).astype(jnp.bfloat16)


def signed(frequency, grid_size):
    return jnp.where(frequency >= grid_size // 2, frequency - grid_size, frequency)


def kernel_table(columns, shift_q, grid_size):
    live_slot = columns >= 0
    column_ids = jnp.where(live_slot, columns, 0)
    freq_x = signed(column_ids % grid_size, grid_size)
    freq_y = signed(column_ids // grid_size, grid_size)
    freq_z = signed(jnp.arange(grid_size, dtype=jnp.int32), grid_size)
    radius = grid_size // 2
    inside = (freq_x * freq_x + freq_y * freq_y)[None, :] + (freq_z * freq_z)[
        :, None
    ] <= radius * radius
    inside = jnp.logical_and(inside, live_slot[None, :])
    wave_x = freq_x.astype(jnp.float32) + shift_q[0]
    wave_y = freq_y.astype(jnp.float32) + shift_q[1]
    wave_z = freq_z.astype(jnp.float32) + shift_q[2]
    square = (wave_z * wave_z)[:, None] + (wave_x * wave_x + wave_y * wave_y)[None, :]
    cell = SPACING_BOHR * grid_size
    exponent = math.pi * math.pi * square / (cell * cell * SCREENING * SCREENING)
    weights = cell * cell / math.pi * -jnp.expm1(-exponent) / square / float(grid_size) ** 3
    return jnp.where(inside, weights, 0.0)


def momentum(kpoint_grid, pool_rank, pool_count):
    pool_rows = jnp.arange(pool_count, dtype=jnp.int32)
    earlier = (pool_rank + pool_count - 1) % pool_count
    current = jnp.sum(jnp.where((pool_rows == pool_rank)[:, None], kpoint_grid, 0), axis=0)
    previous = jnp.sum(jnp.where((pool_rows == earlier)[:, None], kpoint_grid, 0), axis=0)
    return (current - previous).astype(jnp.float32) / KMESH


def pair_density(own_bands, received):
    band_count = own_bands.shape[1]
    real_own = own_bands[0].astype(jnp.float32)[:, None]
    imag_own = own_bands[1].astype(jnp.float32)[:, None]
    real_recv = received[0].astype(jnp.float32)[None]
    imag_recv = received[1].astype(jnp.float32)[None]
    real_part = real_recv * real_own + imag_recv * imag_own
    imag_part = real_recv * imag_own - imag_recv * real_own
    stacked = jnp.stack([real_part, imag_part], axis=2)
    return stacked.reshape((band_count * band_count, 2) + own_bands.shape[2:]).astype(jnp.bfloat16)


def action_of(received, field):
    band_count = received.shape[1]
    field = field.reshape((band_count, band_count) + field.shape[1:])
    real_recv = received[0].astype(jnp.float32)[None]
    imag_recv = received[1].astype(jnp.float32)[None]
    real_field = field[:, :, 0]
    imag_field = field[:, :, 1]
    real_part = -jnp.sum(real_recv * real_field - imag_recv * imag_field, axis=1)
    imag_part = -jnp.sum(real_recv * imag_field + imag_recv * real_field, axis=1)
    return jnp.stack([real_part, imag_part], axis=0).astype(jnp.bfloat16)


def apply_table(data, table, form):
    return jnp.einsum(form, data, table, preferred_element_type=jnp.float32)


def column_pass(picked, weights, forward, backward):
    spectrum = apply_table(picked, forward, "pczs,czdk->pdks")
    scaled = (spectrum * weights).astype(jnp.bfloat16)
    return apply_table(scaled, backward, "pczs,czdk->pdks").astype(jnp.bfloat16)


def local(orbitals, stick_map, kpoint_grid):
    grid_size = NG
    moved = shifted(orbitals, "pool", 1)
    own_bands = orbitals[0].reshape(orbitals.shape[1:4] + (grid_size, grid_size))
    received = moved[0].reshape(orbitals.shape[1:4] + (grid_size, grid_size))
    fft_count = lax.axis_size("fft")
    fft_rank = lax.axis_index("fft")
    pool_count = lax.axis_size("pool")
    pool_rank = lax.axis_index("pool")
    shift_q = momentum(kpoint_grid, pool_rank, pool_count)
    forward = dft_table(grid_size, -1.0)
    backward = dft_table(grid_size, 1.0)
    column_share = grid_size * grid_size // fft_count
    share_ids = fft_rank * column_share + jnp.arange(column_share, dtype=jnp.int32)
    own_rows = fft_rank * (grid_size // fft_count) + jnp.arange(
        grid_size // fft_count, dtype=jnp.int32
    )
    row_hit = (stick_map[None, :] // grid_size == own_rows[:, None]) & (stick_map >= 0)[None, :]
    every_column = jnp.arange(grid_size, dtype=jnp.int32)
    column_hit = stick_map[None, :] % grid_size == every_column[:, None]
    counts = jnp.einsum(
        "rs,cs->rc",
        row_hit.astype(jnp.bfloat16),
        column_hit.astype(jnp.bfloat16),
        preferred_element_type=jnp.float32,
    )
    own_present = counts.reshape(column_share) > 0.5
    weights = kernel_table(jnp.where(own_present, share_ids, -1), shift_q, grid_size)

    def potential(pair_block):
        along_x = apply_table(pair_block, forward, "pczyx,cxek->pezyk").astype(jnp.bfloat16)
        along_y = apply_table(along_x, forward, "pczyx,cyek->pezkx").astype(jnp.bfloat16)
        piece_block = lax.all_to_all(along_y, "fft", split_axis=3, concat_axis=2, tiled=True)
        flat_piece = piece_block.reshape(piece_block.shape[:3] + (column_share,))
        scaled_back = column_pass(flat_piece, weights, forward, backward).reshape(piece_block.shape)
        spectrum = lax.all_to_all(scaled_back, "fft", split_axis=2, concat_axis=3, tiled=True)
        back_y = apply_table(spectrum, backward, "pczkx,ckey->pezyx").astype(jnp.bfloat16)
        return apply_table(back_y, backward, "pczyk,ckex->pezyx")

    density = pair_density(own_bands, received)
    field = lax.map(lambda single_pair: potential(single_pair[None])[0], density)
    result = action_of(received, field)
    return result.reshape((1,) + result.shape[:3] + (grid_size * grid_size,))


def solution(mesh):
    return jax.shard_map(
        local,
        mesh=mesh,
        in_specs=(P("pool", None, None, "fft", None), P(), P()),
        out_specs=P("pool", None, None, "fft", None),
        check_vma=False,
    )
```

profile of v0, /device:TPU:1, one launch (start us, length us, event | category | flops | bytes accessed | tf_op | source)
XLA Modules:
  0.0 118.0 jit_solution(2469198560050355938)
XLA Ops:
  0.0 8.3 %collective-permute-start = (bf16[1,2,1,5,25600]{4,1,3,2,0:T(2,128)(2,1)}, bf16[1,2,1,5,25600]{4,1,3,2,0:T(2,128)(2,1)S(1)}, u32[]{:S(2)}, u32[]{:S(2)}) collective-permute-start(bf16[1,2,1,5,25600]{4,1,3,2,0:T(2,128)(2,1)} %param.3), channel_id=1, source_target_pairs={{0,32},{32,64},{64,96},{96,128},{128,160},{160,192},{192,224},{224... | collective-permute-start | bytes 1536008 | tf_op jit(solution)/shard_map/ppermute | solution.py:16
  8.3 0.9 add_select_fusion.2
  9.2 0.9 broadcast_compare_fusion
  10.1 0.8 select_reduce_fusion
  10.9 0.7 fusion.74
  11.6 0.0 copy-start
  11.6 1.9 %fusion.9 = pred[5,160]{1,0:T(8,128)(4,1)S(1)} fusion(s32[16000]{0:T(1024)S(1)} %get-tuple-element.36, s32[16000]{0:T(1024)S(1)} %get-tuple-element.35, s32[5]{0:T(128)S(1)} %iota_add_fusion, pred[16000]{0:T(1024)(128)(4,1)S(1)} %broadcast_compare_fusion), kind=kOutput, calls=%fused_computation.16 | convolution fusion | flops 28320800 | bytes 144820 | tf_op jit(solution)/shard_map/rs,cs->rc/dot_general | solution.py:117
  13.6 0.1 gt.21
  13.6 0.7 fusion.59
  14.3 0.7 cosine_convert_fusion
  15.0 0.7 negate_convert_fusion.2
  15.7 0.1 fusion.49
  15.7 0.0 copy-start.1
  15.7 16.1 %collective-permute-done = bf16[1,2,1,5,25600]{4,1,3,2,0:T(2,128)(2,1)S(1)} collective-permute-done((bf16[1,2,1,5,25600]{4,1,3,2,0:T(2,128)(2,1)}, bf16[1,2,1,5,25600]{4,1,3,2,0:T(2,128)(2,1)S(1)}, u32[]{:S(2)}, u32[]{:S(2)}) %collective-permute-start) | collective-permute-done | bytes 512032 | tf_op jit(solution)/shard_map/ppermute | solution.py:16
  31.8 0.0 copy-done
  31.8 4.2 %fusion.35 = (bf16[5,25600]{1,0:T(8,128)(2,1)S(1)}, bf16[5,25600]{1,0:T(8,128)(2,1)S(1)}) fusion(bf16[1,2,1,5,25600]{4,1,3,2,0:T(2,128)(2,1)S(1)} %copy-done, bf16[1,2,1,5,25600]{4,1,3,2,0:T(2,128)(2,1)S(1)} %collective-permute-done), kind=kLoop, calls=%fused_computation.53 | loop fusion | flops 1536000 | bytes 1536000 | tf_op jit(solution)/shard_map/convert.5
  36.0 0.5 sub.58
  36.5 0.5 add.242
  37.1 1.0 fusion.7
  38.1 1.8 %copy.79 = bf16[1,2,5,160,160]{4,1,2,0,3:T(2,128)(2,1)} copy(bf16[1,2,5,160,160]{4,3,2,1,0:T(8,128)(2,1)S(1)} %fusion.7) | data formatting | bytes 1024000 | tf_op jit(solution)/shard_map/while/body/eval_jaxpr/convert_element_type | solution.py:128
  39.9 0.0 copy-done.1
  39.9 13.5 %all-to-all-start = ((bf16[1,2,5,160,160]{4,1,2,0,3:T(2,128)(2,1)}), bf16[1,2,5,160,160]{4,1,2,0,3:T(2,128)(2,1)S(1)}, u32[]{:S(2)}, u32[]{:S(2)}) async-start(bf16[1,2,5,160,160]{4,1,2,0,3:T(2,128)(2,1)} %copy.79), calls=%async_computation | async-start | bytes 1638400 | tf_op jit(solution)/shard_map/while/body/eval_jaxpr/all_to_all | solution.py:129
  53.3 0.6 add_multiply_fusion.1
  53.9 1.3 %multiply_add_fusion = f32[800]{0:T(1024)S(1)} fusion(f32[]{:T(128)} %bitcast.30, f32[]{:T(128)} %bitcast.29, pred[800]{0:T(1024)(128)(4,1)S(1)} %gt.21, s32[]{:T(128)S(6)} %mul.330), kind=kLoop, calls=%fused_computation.98 | loop fusion | flops 23200 | bytes 4012 | tf_op jit(solution)/shard_map/add | solution.py:48
  55.2 0.5 fusion.21
  55.8 20.6 %all-to-all-done = bf16[1,2,5,160,160]{4,1,2,0,3:T(2,128)(2,1)S(1)} async-done(((bf16[1,2,5,160,160]{4,1,2,0,3:T(2,128)(2,1)}), bf16[1,2,5,160,160]{4,1,2,0,3:T(2,128)(2,1)S(1)}, u32[]{:S(2)}, u32[]{:S(2)}) %all-to-all-start) | async-done | bytes 512032 | tf_op jit(solution)/shard_map/while/body/eval_jaxpr/all_to_all | solution.py:129
  76.3 0.6 copy.80
  76.9 0.2 copy.81
  77.1 1.1 reshape.574
  78.2 1.8 %fusion.4 = bf16[2,160,800]{2,1,0:T(8,128)(2,1)S(1)} fusion(bf16[2,160,800,1]{2,1,0,3:T(8,128)(2,1)S(1)} %reshape.574, f32[160,800]{1,0:T(8,128)S(1)} %fusion.21, bf16[1,160,2,160]{1,3,0,2:T(8,128)(2,1)S(1)} %get-tuple-element.32, bf16[1,160,2,160]{1,3,0,2:T(8,128)(2,1)} %copy-done.1, bf16[1,160,2,160]{1,3,2,0:T(8,128)(2,1)S(1)} %get-tuple-element.34, ...), kind=kOutput, calls=%fused_computation.11 | convolution fusion | flops 328652800 | bytes 1945600 | tf_op jit(solution)/shard_map/while/body/eval_jaxpr/pczs,czdk->pdks/dot_general | solution.py:88
  80.0 0.3 copy.82
  80.3 1.7 %copy.83 = bf16[1,2,160,5,160]{4,1,3,0,2:T(2,128)(2,1)S(1)} copy(bf16[1,2,160,5,160]{2,4,3,1,0:T(8,128)(2,1)S(1)} %bitcast.188) | data formatting | bytes 1024000 | tf_op jit(solution)/shard_map/while/body/eval_jaxpr/reshape | solution.py:131
  82.0 26.6 %all_to_all.38 = bf16[1,2,160,5,160]{4,1,3,0,2:T(2,128)(2,1)S(1)} all-to-all(bf16[1,2,160,5,160]{4,1,3,0,2:T(2,128)(2,1)S(1)} %copy.83), channel_id=1, replica_groups=mesh['pool'=16,'fft'=32] {'fft'}, dimensions={2} | all-to-all | bytes 1024000 | tf_op jit(solution)/shard_map/while/body/eval_jaxpr/all_to_all | solution.py:132
  108.6 0.6 copy.84
  109.2 0.6 fusion.6
  109.8 0.6 convolution_bitcast_fusion
  110.4 0.1 fusion.73
  110.5 0.4 copy.90
  110.9 0.9 squeeze.29
  111.9 0.4 copy.89
  112.3 0.9 squeeze.28
  113.2 1.8 %negate_convert_fusion.1 = (bf16[1,1,1,5,25600]{4,2,3,1,0:T(2,128)(2,1)S(1)}, bf16[1,1,1,5,25600]{4,2,3,1,0:T(2,128)(2,1)S(1)}) fusion(f32[1,1,1,5,25600]{4,2,3,1,0:T(1,128)S(1)} %squeeze.29, f32[1,1,1,5,25600]{4,2,3,1,0:T(1,128)S(1)} %squeeze.28, bf16[1,2,1,5,25600]{4,1,3,2,0:T(2,128)(2,1)S(1)} %collective-permute-done), kind=kLoop, calls=%fused_computation.51 | loop fusion | flops 1536000 | bytes 2048000 | tf_op jit(solution)/shard_map/convert
  115.0 1.7 %pad_maximum_fusion = bf16[1,2,1,5,25600]{4,2,3,1,0:T(2,128)(2,1)S(1)} fusion(bf16[1,1,1,5,25600]{4,2,3,1,0:T(2,128)(2,1)S(1)} %get-tuple-element.30, bf16[1,1,1,5,25600]{4,2,3,1,0:T(2,128)(2,1)S(1)} %get-tuple-element.29), kind=kLoop, calls=%fused_computation.17 | loop fusion | flops 256000 | bytes 1024000 | tf_op jit(solution)/shard_map/stack | solution.py:84
  116.7 1.3 %copy.91 = bf16[1,2,1,5,25600]{4,1,3,2,0:T(2,128)(2,1)} copy(bf16[1,2,1,5,25600]{4,2,3,1,0:T(2,128)(2,1)S(1)} %pad_maximum_fusion) | data formatting | bytes 1024000 | tf_op jit(solution)/shard_map/stack | solution.py:84
  (6 shorter events, 0.1 us)
Async XLA Ops:
  0.0 31.8 %collective-permute-start = (bf16[1,2,1,5,25600]{4,1,3,2,0:T(2,128)(2,1)}, bf16[1,2,1,5,25600]{4,1,3,2,0:T(2,128)(2,1)S(1)}, u32[]{:S(2)}, u32[]{:S(2)}) collective-permute-start(bf16[1,2,1,5,25600]{4,1,3,2,0:T(2,128)(2,1)} %param.3), channel_id=1, source_target_pairs={{0,32},{32,64},{64,96},{96,128},{128,160},{160,192},{192,224},{224... | collective-permute-start | bytes 1536008 | tf_op jit(solution)/shard_map/ppermute | solution.py:16
  11.6 20.2 %copy-start = (bf16[1,2,1,5,25600]{4,1,3,2,0:T(2,128)(2,1)S(1)}, bf16[1,2,1,5,25600]{4,1,3,2,0:T(2,128)(2,1)}, u32[]{:S(2)}) copy-start(bf16[1,2,1,5,25600]{4,1,3,2,0:T(2,128)(2,1)} %param.3) | copy-start | bytes 1536004
  15.7 24.1 %copy-start.1 = (bf16[1,160,2,160]{1,3,0,2:T(8,128)(2,1)}, bf16[1,160,2,160]{1,3,0,2:T(8,128)(2,1)S(1)}, u32[]{:S(2)}) copy-start(bf16[1,160,2,160]{1,3,0,2:T(8,128)(2,1)S(1)} %get-tuple-element.33) | copy-start | bytes 307204
  39.9 36.5 %all-to-all-start = ((bf16[1,2,5,160,160]{4,1,2,0,3:T(2,128)(2,1)}), bf16[1,2,5,160,160]{4,1,2,0,3:T(2,128)(2,1)S(1)}, u32[]{:S(2)}, u32[]{:S(2)}) async-start(bf16[1,2,5,160,160]{4,1,2,0,3:T(2,128)(2,1)} %copy.79), calls=%async_computation | async-start | bytes 1638400 | tf_op jit(solution)/shard_map/while/body/eval_jaxpr/all_to_all | solution.py:129
where the time goes:
time: 118 us
  waiting for transfers between devices  36.6 us (31%)
  blocking collectives  26.6 us (23%)
  starting transfers between devices  21.7 us (18%)
  other arithmetic  14.8 us (13%)
  local copies, waits for them, and re-layouts  12.1 us (10%)
  matrix products  5.98 us (5%)
    all_to_all x1, blocking collectives, potential(): lax.all_to_all(scaled_back, 'fft', split_axis=2, concat_axis=3, tiled=True)  26.6 us
    all_to_all x1, waiting for transfers between devices, potential(): lax.all_to_all(along_y, 'fft', split_axis=3, concat_axis=2, tiled=True)  20.6 us
    ppermute x1, waiting for transfers between devices, shifted(): return lax.ppermute(value, axis, pairs)  16.1 us
    all_to_all x1, starting transfers between devices, potential(): lax.all_to_all(along_y, 'fft', split_axis=3, concat_axis=2, tiled=True)  13.5 us
    ppermute x1, starting transfers between devices, shifted(): return lax.ppermute(value, axis, pairs)  8.26 us
    another operation x5, other arithmetic  7.94 us
    dot_general x4, matrix products, apply_table(): return jnp.einsum(form, data, table, preferred_element_type=jnp.float32)  4.06 us
  transfers between devices with their start and end apart: 2, of which 2 were waited for; matrix products, arithmetic and copies ran while one was open for 8% of the time, Pallas kernels for 0%

commit v1 on v0

--- a/solution.py
+++ b/solution.py
@@ -129,7 +129,16 @@
         piece_block = lax.all_to_all(along_y, "fft", split_axis=3, concat_axis=2, tiled=True)
         flat_piece = piece_block.reshape(piece_block.shape[:3] + (column_share,))
         scaled_back = column_pass(flat_piece, weights, forward, backward).reshape(piece_block.shape)
-        spectrum = lax.all_to_all(scaled_back, "fft", split_axis=2, concat_axis=3, tiled=True)
+        remake_table_up = lambda x_in: jnp.concatenate(
+            lax.all_to_all(
+                jnp.stack(jnp.split(x_in, lax.psum(1, axis_name="fft"), axis=2)),
+                axis_name="fft",
+                split_axis=0,
+                concat_axis=0,
+            ),
+            axis=3,
+        )
+        spectrum = remake_table_up(scaled_back)
         back_y = apply_table(spectrum, backward, "pczkx,ckey->pezyx").astype(jnp.bfloat16)
         return apply_table(back_y, backward, "pczyk,ckex->pezyx")
 

time: 118 us -> 161 us (1.36)
  local copies, waits for them, and re-layouts: 12.1 us -> 53 us
    unnamed x4 -> x35, local copies, waits for them, and re-layouts: 0.01 us -> 29.1 us
    another operation x1 -> x3, local copies, waits for them, and re-layouts: 1.07 us -> 14.6 us  [the longest x2 13.5 us: potential(): jnp.stack(jnp.split(x_in, lax.psum(1, axis_name='fft'), axis=2))]
  transfers between devices with their start and end apart: 2 -> 2, of which waited for: 2 -> 2; matrix products, arithmetic and copies ran while one was open for 8% -> 6% of each run, Pallas kernels for 0% -> 0%
where the time goes in v1:
time: 161 us; the launch traced here: 160 us
  local copies, waits for them, and re-layouts  53 us (33%)
  waiting for transfers between devices  36.5 us (23%)
  blocking collectives  26.6 us (17%)
  starting transfers between devices  21.7 us (13%)
  other arithmetic  16 us (10%)
  matrix products  6.05 us (4%)
    unnamed x35, local copies, waits for them, and re-layouts  29.1 us
    all_to_all x1, blocking collectives, potential(): lax.all_to_all(jnp.stack(jnp.split(x_in, lax.psum(1, axis_name='fft'), ax...  26.6 us
    all_to_all x1, waiting for transfers between devices, potential(): lax.all_to_all(along_y, 'fft', split_axis=3, concat_axis=2, tiled=True)  20.5 us
    ppermute x1, waiting for transfers between devices, shifted(): return lax.ppermute(value, axis, pairs)  16 us
    another operation x2, local copies, waits for them, and re-layouts, potential(): jnp.stack(jnp.split(x_in, lax.psum(1, axis_name='fft'), axis=2))  13.5 us
    all_to_all x1, starting transfers between devices, potential(): lax.all_to_all(along_y, 'fft', split_axis=3, concat_axis=2, tiled=True)  13.5 us
    another operation x5, other arithmetic  9.1 us
    ppermute x1, starting transfers between devices, shifted(): return lax.ppermute(value, axis, pairs)  8.26 us
  transfers between devices with their start and end apart: 2, of which 2 were waited for; matrix products, arithmetic and copies ran while one was open for 6% of the time, Pallas kernels for 0%

profile of v1, /device:TPU:1, one launch (start us, length us, event | category | flops | bytes accessed | tf_op | source)
XLA Modules:
  0.0 160.2 jit_solution(4685730104756746464)
XLA Ops:
  0.0 8.3 %collective-permute-start = (bf16[1,2,1,5,25600]{4,1,3,2,0:T(2,128)(2,1)}, bf16[1,2,1,5,25600]{4,1,3,2,0:T(2,128)(2,1)S(1)}, u32[]{:S(2)}, u32[]{:S(2)}) collective-permute-start(bf16[1,2,1,5,25600]{4,1,3,2,0:T(2,128)(2,1)} %param.3), channel_id=1, source_target_pairs={{0,32},{32,64},{64,96},{96,128},{128,160},{160,192},{192,224},{224... | collective-permute-start | bytes 1536008 | tf_op jit(solution)/shard_map/ppermute | solution.py:16
  11.6 1.9 %fusion.9 = pred[5,160]{1,0:T(8,128)(4,1)S(1)} fusion(s32[16000]{0:T(1024)S(1)} %get-tuple-element.36, s32[16000]{0:T(1024)S(1)} %get-tuple-element.35, s32[5]{0:T(128)S(1)} %iota_add_fusion, pred[16000]{0:T(1024)(128)(4,1)S(1)} %broadcast_compare_fusion), kind=kOutput, calls=%fused_computation.16 | convolution fusion | flops 28320800 | bytes 144820 | tf_op jit(solution)/shard_map/rs,cs->rc/dot_general | solution.py:117
  15.8 16.0 %collective-permute-done = bf16[1,2,1,5,25600]{4,1,3,2,0:T(2,128)(2,1)S(1)} collective-permute-done((bf16[1,2,1,5,25600]{4,1,3,2,0:T(2,128)(2,1)}, bf16[1,2,1,5,25600]{4,1,3,2,0:T(2,128)(2,1)S(1)}, u32[]{:S(2)}, u32[]{:S(2)}) %collective-permute-start) | collective-permute-done | bytes 512032 | tf_op jit(solution)/shard_map/ppermute | solution.py:16
  31.8 5.3 %fusion.35 = (bf16[5,25600]{1,0:T(8,128)(2,1)S(1)}, bf16[5,25600]{1,0:T(8,128)(2,1)S(1)}) fusion(bf16[1,2,1,5,25600]{4,1,3,2,0:T(2,128)(2,1)} %param.3, bf16[1,2,1,5,25600]{4,1,3,2,0:T(2,128)(2,1)S(1)} %collective-permute-done), kind=kLoop, calls=%fused_computation.53 | loop fusion | flops 1536000 | bytes 1536000 | tf_op jit(solution)/shard_map/convert.5
  38.2 1.0 fusion.7
  39.3 1.8 %copy.144 = bf16[1,2,5,160,160]{4,1,2,0,3:T(2,128)(2,1)} copy(bf16[1,2,5,160,160]{4,3,2,1,0:T(8,128)(2,1)S(1)} %fusion.7) | data formatting | bytes 1024000 | tf_op jit(solution)/shard_map/while/body/eval_jaxpr/convert_element_type | solution.py:128
  41.0 13.5 %all-to-all-start = ((bf16[1,2,5,160,160]{4,1,2,0,3:T(2,128)(2,1)}), bf16[1,2,5,160,160]{4,1,2,0,3:T(2,128)(2,1)S(1)}, u32[]{:S(2)}, u32[]{:S(2)}) async-start(bf16[1,2,5,160,160]{4,1,2,0,3:T(2,128)(2,1)} %copy.144), calls=%async_computation | async-start | bytes 1638400 | tf_op jit(solution)/shard_map/while/body/eval_jaxpr/all_to_all | solution.py:129
  55.2 1.2 multiply_add_fusion
  57.0 20.5 %all-to-all-done = bf16[1,2,5,160,160]{4,1,2,0,3:T(2,128)(2,1)S(1)} async-done(((bf16[1,2,5,160,160]{4,1,2,0,3:T(2,128)(2,1)}), bf16[1,2,5,160,160]{4,1,2,0,3:T(2,128)(2,1)S(1)}, u32[]{:S(2)}, u32[]{:S(2)}) %all-to-all-start) | async-done | bytes 512032 | tf_op jit(solution)/shard_map/while/body/eval_jaxpr/all_to_all | solution.py:129
  78.3 1.1 reshape.581
  79.4 1.9 %fusion.4 = bf16[2,160,800]{2,1,0:T(8,128)(2,1)S(1)} fusion(bf16[2,160,800,1]{2,1,0,3:T(8,128)(2,1)S(1)} %reshape.581, f32[160,800]{1,0:T(8,128)S(1)} %fusion.21, bf16[1,160,2,160]{1,3,0,2:T(8,128)(2,1)} %copy-done, bf16[1,160,2,160]{1,3,0,2:T(8,128)(2,1)} %copy-done.1, bf16[1,160,2,160]{1,3,2,0:T(8,128)(2,1)S(1)} %get-tuple-element.34, ...), kind=kOutput, calls=%fused_computation.11 | convolution fusion | flops 328652800 | bytes 1945600 | tf_op jit(solution)/shard_map/while/body/eval_jaxpr/pczs,czdk->pdks/dot_general | solution.py:88
  82.4 0.9 fusion.68
  83.3 0.9 fusion.67
  84.3 0.9 fusion.66
  85.2 0.9 fusion.65
  86.2 0.9 fusion.64
  87.1 0.9 fusion.63
  88.0 0.9 fusion.62
  89.0 0.9 fusion.61
  89.9 0.9 fusion.60
  90.8 0.9 fusion.59
  91.8 0.9 fusion.58
  92.7 0.9 fusion.57
  93.6 1.0 fusion.56
  94.6 0.9 fusion.55
  95.5 0.9 fusion.54
  96.5 0.9 fusion.53
  97.4 0.9 fusion.52
  98.3 0.9 fusion.51
  99.3 0.9 fusion.50
  100.2 1.0 fusion.49
  101.2 1.0 fusion.48
  102.2 1.0 fusion.47
  104.1 0.9 fusion.45
  105.0 0.9 fusion.44
  105.9 1.0 fusion.43
  106.9 1.0 fusion.42
  107.9 0.9 fusion.41
  108.8 0.9 fusion.40
  109.7 0.9 fusion.39
  110.7 1.0 fusion.38
  111.6 12.6 %copy.148 = bf16[32,1,2,5,5,160]{5,2,4,3,1,0:T(2,128)(2,1)S(1)} copy(bf16[32,1,2,5,5,160]{3,5,4,2,1,0:T(8,128)(2,1)} %fusion.38) | data formatting | bytes 1024000 | tf_op jit(solution)/shard_map/while/body/eval_jaxpr/stack | solution.py:134
  124.2 26.6 %all_to_all.25 = bf16[32,1,2,5,5,160]{5,2,4,3,1,0:T(2,128)(2,1)S(1)} all-to-all(bf16[32,1,2,5,5,160]{5,2,4,3,1,0:T(2,128)(2,1)S(1)} %copy.148), channel_id=1, replica_groups=mesh['pool'=16,'fft'=32] {'fft'}, dimensions={0} | all-to-all | bytes 1024000 | tf_op jit(solution)/shard_map/while/body/eval_jaxpr/all_to_all | solution.py:133
  153.1 0.9 squeeze.29
  154.4 0.9 squeeze.28
  155.4 1.8 %negate_convert_fusion.1 = (bf16[1,1,1,5,25600]{4,2,3,1,0:T(2,128)(2,1)S(1)}, bf16[1,1,1,5,25600]{4,2,3,1,0:T(2,128)(2,1)S(1)}) fusion(f32[1,1,1,5,25600]{4,2,3,1,0:T(1,128)S(1)} %squeeze.29, f32[1,1,1,5,25600]{4,2,3,1,0:T(1,128)S(1)} %squeeze.28, bf16[1,2,1,5,25600]{4,1,3,2,0:T(2,128)(2,1)S(1)} %collective-permute-done), kind=kLoop, calls=%fused_computation.51 | loop fusion | flops 1536000 | bytes 2048000 | tf_op jit(solution)/shard_map/convert
  157.2 1.7 %pad_maximum_fusion = bf16[1,2,1,5,25600]{4,2,3,1,0:T(2,128)(2,1)S(1)} fusion(bf16[1,1,1,5,25600]{4,2,3,1,0:T(2,128)(2,1)S(1)} %get-tuple-element.30, bf16[1,1,1,5,25600]{4,2,3,1,0:T(2,128)(2,1)S(1)} %get-tuple-element.29), kind=kLoop, calls=%fused_computation.17 | loop fusion | flops 256000 | bytes 1024000 | tf_op jit(solution)/shard_map/stack | solution.py:84
  158.9 1.3 copy.156
  (34 shorter events, 13.3 us)
Async XLA Ops:
  0.0 31.8 %collective-permute-start = (bf16[1,2,1,5,25600]{4,1,3,2,0:T(2,128)(2,1)}, bf16[1,2,1,5,25600]{4,1,3,2,0:T(2,128)(2,1)S(1)}, u32[]{:S(2)}, u32[]{:S(2)}) collective-permute-start(bf16[1,2,1,5,25600]{4,1,3,2,0:T(2,128)(2,1)} %param.3), channel_id=1, source_target_pairs={{0,32},{32,64},{64,96},{96,128},{128,160},{160,192},{192,224},{224... | collective-permute-start | bytes 1536008 | tf_op jit(solution)/shard_map/ppermute | solution.py:16
  15.8 62.3 %copy-start = (bf16[1,160,2,160]{1,3,0,2:T(8,128)(2,1)}, bf16[1,160,2,160]{1,3,0,2:T(8,128)(2,1)S(1)}, u32[]{:S(2)}) copy-start(bf16[1,160,2,160]{1,3,0,2:T(8,128)(2,1)S(1)} %get-tuple-element.32) | copy-start | bytes 307204
  15.8 62.3 %copy-start.1 = (bf16[1,160,2,160]{1,3,0,2:T(8,128)(2,1)}, bf16[1,160,2,160]{1,3,0,2:T(8,128)(2,1)S(1)}, u32[]{:S(2)}) copy-start(bf16[1,160,2,160]{1,3,0,2:T(8,128)(2,1)S(1)} %get-tuple-element.33) | copy-start | bytes 307204
  41.0 36.5 %all-to-all-start = ((bf16[1,2,5,160,160]{4,1,2,0,3:T(2,128)(2,1)}), bf16[1,2,5,160,160]{4,1,2,0,3:T(2,128)(2,1)S(1)}, u32[]{:S(2)}, u32[]{:S(2)}) async-start(bf16[1,2,5,160,160]{4,1,2,0,3:T(2,128)(2,1)} %copy.144), calls=%async_computation | async-start | bytes 1638400 | tf_op jit(solution)/shard_map/while/body/eval_jaxpr/all_to_all | solution.py:129
